TPU v7x, 32 devices: a whole 2x2x4 slice. The times are simulated.
32 devices in a mesh: dp: 8 (over y, x, core), expert: 4 (over z).
Axes of the slice: x: 2, y: 2, z: 4, core: 2. Of those that a mesh axis runs over, the one named last changes fastest.
Arguments:
- hidden_states: bfloat16 [4, 8192, 4096], P(None, ('dp', 'expert')), may hold values from -8 to 8
- router_weight: bfloat16 [4, 8, 4096], replicated, may hold values from -0.125 to 0.125
- expert_ids: int32 [4, 8192, 2], P(None, ('dp', 'expert')), may hold values from 0 to 7, as said below
Outputs:
- router_grad: float32 [4, 8, 4096], P(None, None, 'dp')
- losses: float32 [4, 2], replicated
Inputs may be any that keep to these rules, and one draw needn't show every extreme that they name: `expert_ids`: each token names 2 different experts in each layer.
All inputs are finite; a program needn't handle non-finite values.
Results may differ from a plain program's by a relative error of at most 0.0018.
Values sent between devices are 32-bit elements; how exact they have to be, the bound alone decides.
A program may use at most 64 MiB of HBM per device.

v0:
```python
import jax
import jax.numpy as jnp
from jax import lax
from jax.sharding import PartitionSpec as P

balance_coef = 0.02
zloss_coef = 0.001


def local_counts(chosen, experts):
    labels = jnp.arange(experts, dtype=jnp.int32)[:, None]
    counts = jnp.zeros((experts,), jnp.float32)
    for slot in range(chosen.shape[1]):
        counts = counts + jnp.sum((chosen[:, slot][None, :] == labels).astype(jnp.float32), axis=1)
    return counts


def on_device(hidden_states, router_weight, expert_ids):
    layers = hidden_states.shape[0]
    rows = hidden_states.shape[1]
    experts = router_weight.shape[1]
    picks = expert_ids.shape[2]
    tokens_all = rows * lax.axis_size("dp") * lax.axis_size("expert")
    terms = []
    count_list = []
    prob_sums = []
    square_sums = []
    for layer in range(layers):
        states = hidden_states[layer]
        logits = lax.dot_general(
            router_weight[layer],
            states,
            (((1,), (1,)), ((), ())),
            preferred_element_type=jnp.float32,
        )
        expo = jnp.exp(logits)
        total = jnp.sum(expo, axis=0)
        probs = expo / total[None, :]
        lse = jnp.log(total)
        prob_sums.append(jnp.sum(probs, axis=1))
        square_sums.append(jnp.sum(lse * lse))
        counts = lax.psum(local_counts(expert_ids[layer], experts), ("dp", "expert"))
        count_list.append(counts)
        share = counts / (tokens_all * picks)
        pull = balance_coef * experts * share
        mixed = jnp.sum(probs * pull[:, None], axis=0)
        dlogits = probs * (pull[:, None] - mixed[None, :]) + 2.0 * zloss_coef * lse[None, :] * probs
        dlogits = dlogits.astype(jnp.bfloat16)
        term = jnp.dot(dlogits, states, preferred_element_type=jnp.float32)
        terms.append(term)
    columns = lax.psum_scatter(jnp.stack(terms), "dp", scatter_dimension=2, tiled=True)
    router_grad = lax.psum(columns, "expert")
    prob_total, square_total = lax.psum(
        (jnp.stack(prob_sums), jnp.stack(square_sums)), ("dp", "expert")
    )
    share_table = jnp.stack(count_list) / (tokens_all * picks)
    balance = experts * jnp.sum(share_table * prob_total / tokens_all, axis=1)
    zloss = square_total / tokens_all
    return (router_grad, jnp.stack([balance, zloss], axis=-1))


def solution(mesh):
    in_specs = (P(None, ("dp", "expert"), None), P(), P(None, ("dp", "expert"), None))
    out_specs = (P(None, None, "dp"), P())
    return jax.shard_map(
        on_device, mesh=mesh, in_specs=in_specs, out_specs=out_specs, check_vma=False
    )
```

profile of v0, /device:TPU:0, one launch (start us, length us, event | category | flops | bytes accessed | tf_op | source)
XLA Modules:
  0.0 158.2 jit_solution(140643967143512886)
XLA Ops:
  7.2 0.0 reduce-scatter.2.cloned.1.call-start
  7.2 2.3 %fusion.65 = (f32[256]{0:T(256)S(1)}, f32[8,256]{1,0:T(8,128)S(1)}) fusion(bf16[4,256,4096]{2,1,0:T(8,128)(2,1)} %param.3, bf16[4,8,4096]{2,1,0:T(8,128)(2,1)} %param.4), kind=kOutput, calls=%fused_computation.112 | convolution fusion | flops 16779008 | bytes 2171904 | tf_op jit(solution)/shard_map/dot_general | solution.py:30
  9.5 2.3 %fusion.66 = (f32[256]{0:T(256)S(1)}, f32[8,256]{1,0:T(8,128)S(1)}) fusion(bf16[4,256,4096]{2,1,0:T(8,128)(2,1)} %param.3, bf16[4,8,4096]{2,1,0:T(8,128)(2,1)} %param.4), kind=kOutput, calls=%fused_computation.113 | convolution fusion | flops 16779008 | bytes 2171904 | tf_op jit(solution)/shard_map/dot_general | solution.py:30
  11.8 2.3 %fusion.63 = (f32[256]{0:T(256)S(1)}, f32[8,256]{1,0:T(8,128)S(1)}) fusion(bf16[4,256,4096]{2,1,0:T(8,128)(2,1)} %param.3, bf16[4,8,4096]{2,1,0:T(8,128)(2,1)} %param.4), kind=kOutput, calls=%fused_computation.110 | convolution fusion | flops 16779008 | bytes 2171904 | tf_op jit(solution)/shard_map/dot_general | solution.py:30
  14.1 0.7 slice_bitcast_fusion.3
  14.9 0.1 convert_reduce_fusion.6
  15.0 0.1 convert_reduce_fusion.7
  15.1 0.1 convert_reduce_fusion.4
  15.2 0.1 convert_reduce_fusion.5
  15.4 0.1 convert_reduce_fusion
  15.5 0.1 convert_reduce_fusion.1
  15.6 0.1 convert_reduce_fusion.2
  15.7 0.1 convert_reduce_fusion.3
  15.9 2.3 %fusion.64 = (f32[256]{0:T(256)S(1)}, f32[8,256]{1,0:T(8,128)S(1)}) fusion(bf16[4,256,4096]{2,1,0:T(8,128)(2,1)} %param.3, bf16[4,8,4096]{2,1,0:T(8,128)(2,1)} %param.4), kind=kOutput, calls=%fused_computation.111 | convolution fusion | flops 16779008 | bytes 2171904 | tf_op jit(solution)/shard_map/dot_general | solution.py:30
  18.2 42.0 %all-reduce.1 = (f32[8]{0:T(128)S(1)}, f32[8]{0:T(128)S(1)}, f32[8]{0:T(128)S(1)}, f32[8]{0:T(128)S(1)}) all-reduce(f32[8]{0:T(128)S(1)} %add.46, f32[8]{0:T(128)S(1)} %add.44, f32[8]{0:T(128)S(1)} %add.42, f32[8]{0:T(128)S(1)} %add.40), channel_id=1, replica_groups=mesh['dp'=8,'expert'=4] {'dp','expert'}, use_global_device_ids=true, to_apply=%region_18.0 | all-reduce | flops 32 | bytes 256 | tf_op jit(solution)/shard_map/psum | solution.py:42
  60.2 0.6 multiply_reduce_fusion.6
  60.8 0.7 multiply_reduce_fusion.7
  61.5 0.6 multiply_reduce_fusion.4
  62.1 0.6 multiply_reduce_fusion.5
  62.7 0.2 fusion.55
  62.9 2.0 %convolution_bitcast_fusion.3 = f32[1,8,4096]{2,1,0:T(8,128)S(1)} fusion(bf16[4,256,4096]{2,1,0:T(8,128)(2,1)} %param.3, f32[256]{0:T(256)S(1)} %get-tuple-element.29, f32[256]{0:T(256)S(1)} %get-tuple-element.3, f32[8]{0:T(128)S(1)} %broadcast_multiply_fusion.3, f32[8,256]{1,0:T(8,128)S(1)} %get-tuple-element.43, f32[256]{0:T(256)S(1)} %get-tuple-element.42), kind=kOutput, calls=%fused_computation.3 | convolution fusion | flops 16787456 | bytes 2239520 | tf_op jit(solution)/shard_map/dot_general | solution.py:49
  64.9 2.0 %convolution_bitcast_fusion.2 = f32[1,8,4096]{2,1,0:T(8,128)S(1)} fusion(bf16[4,256,4096]{2,1,0:T(8,128)(2,1)} %param.3, f32[256]{0:T(256)S(1)} %get-tuple-element.31, f32[256]{0:T(256)S(1)} %get-tuple-element.44, f32[8]{0:T(128)S(1)} %broadcast_multiply_fusion.2, f32[8,256]{1,0:T(8,128)S(1)} %get-tuple-element.41, f32[256]{0:T(256)S(1)} %get-tuple-element.40), kind=kOutput, calls=%fused_computation.2 | convolution fusion | flops 16787456 | bytes 2239520 | tf_op jit(solution)/shard_map/dot_general | solution.py:49
  66.9 0.2 fusion.57
  67.1 2.0 %convolution_bitcast_fusion.1 = f32[1,8,4096]{2,1,0:T(8,128)S(1)} fusion(bf16[4,256,4096]{2,1,0:T(8,128)(2,1)} %param.3, f32[256]{0:T(256)S(1)} %get-tuple-element.33, f32[256]{0:T(256)S(1)} %get-tuple-element.7, f32[8]{0:T(128)S(1)} %broadcast_multiply_fusion.1, f32[8,256]{1,0:T(8,128)S(1)} %get-tuple-element.39, f32[256]{0:T(256)S(1)} %get-tuple-element.38), kind=kOutput, calls=%fused_computation.1 | convolution fusion | flops 16787456 | bytes 2239520 | tf_op jit(solution)/shard_map/dot_general | solution.py:49
  69.1 2.0 %convolution_bitcast_fusion = f32[1,8,4096]{2,1,0:T(8,128)S(1)} fusion(bf16[4,256,4096]{2,1,0:T(8,128)(2,1)} %param.3, f32[256]{0:T(256)S(1)} %get-tuple-element.35, f32[256]{0:T(256)S(1)} %get-tuple-element.46, f32[8]{0:T(128)S(1)} %broadcast_multiply_fusion, f32[8,256]{1,0:T(8,128)S(1)} %get-tuple-element.37, f32[256]{0:T(256)S(1)} %get-tuple-element.36), kind=kOutput, calls=%fused_computation | convolution fusion | flops 16787456 | bytes 2239520 | tf_op jit(solution)/shard_map/dot_general | solution.py:49
  71.1 0.8 pad_maximum_fusion
  71.9 0.0 reduce-scatter.2.cloned.1.call-update
  71.9 0.0 all-reduce.4.cloned.1.call-start
  72.0 2.6 %pad_maximum_fusion.3 = f32[4]{0:T(128)S(1)} fusion(f32[1]{0:T(128)} %bitcast.36, f32[1]{0:T(128)} %bitcast.35, f32[1]{0:T(128)} %bitcast.34, f32[1]{0:T(128)} %bitcast.33), kind=kLoop, calls=%fused_computation.95 | loop fusion | flops 12 | bytes 32 | tf_op jit(solution)/shard_map/stack | solution.py:54
  74.6 40.0 %all-reduce = (f32[4]{0:T(128)S(1)}, f32[4,8]{1,0:T(4,128)S(1)}) all-reduce(f32[4]{0:T(128)S(1)} %pad_maximum_fusion.3, f32[4,8]{1,0:T(4,128)S(1)} %pad_maximum_fusion.1), channel_id=1, replica_groups=mesh['dp'=8,'expert'=4] {'dp','expert'}, use_global_device_ids=true, to_apply=%region_32.0 | all-reduce | flops 36 | bytes 288 | tf_op jit(solution)/shard_map/psum | solution.py:53
  114.7 0.1 fusion.54
  114.8 0.0 reduce-scatter.2.cloned.1.call-done
  114.8 0.0 all-reduce.4.cloned.1.call-update
  114.8 0.6 pad_maximum_fusion.2
  115.4 34.5 %all-reduce.4.cloned.1.call-done = f32[4,8,512]{2,1,0:T(8,128)} async-done(((f32[4,8,512]{2,1,0:T(8,128)}), f32[4,8,512]{2,1,0:T(8,128)}) %all-reduce.4.cloned.1.call-update) | async-done | bytes 65552 | tf_op jit(solution)/shard_map/psum | solution.py:52
  149.9 1.5 copy.6
  (15 shorter events, 0.1 us)
Async XLA Ops:
  7.2 107.6 %reduce-scatter.2.cloned.1.call-start = ((), (), s32[]{:S(2)}) async-start(), calls=%async_computation.1 | async-start | bytes 589824 | tf_op jit(solution)/shard_map/reduce_scatter | solution.py:51
  71.9 78.0 %all-reduce.4.cloned.1.call-start = ((), (), s32[]{:S(2)}) async-start(), calls=%async_computation.2 | async-start | bytes 131072 | tf_op jit(solution)/shard_map/psum | solution.py:52
Sparse Core Ops, SparseCore 0:
  72.1 33.9 reduce-scatter.1
  115.0 34.9 all-reduce.3
where the time goes:
time: 159 us; the launch traced here: 158 us
  blocking collectives  82.1 us (52%)
  waiting for transfers between devices  34.6 us (22%)
  matrix products  17.3 us (11%)
  between operations  14.2 us (9%)
  other arithmetic  7.88 us (5%)
  local copies, waits for them, and re-layouts  2.23 us (1%)
    psum x1, blocking collectives, on_device(): lax.psum(local_counts(expert_ids[layer], experts), ('dp', 'expert'))  42 us
    psum x1, blocking collectives, on_device(): lax.psum((jnp.stack(prob_sums), jnp.stack(square_sums)), ('dp', 'expert'))  40 us
    psum x1, waiting for transfers between devices, on_device(): router_grad = lax.psum(columns, 'expert')  34.5 us
    dot_general x4, matrix products, on_device(): lax.dot_general(router_weight[layer], states, (((1,), (1,)), ((), ())), p...  9.21 us
    dot_general x4, matrix products, on_device(): term = jnp.dot(dlogits, states, preferred_element_type=jnp.float32)  8.06 us
  transfers between devices with their start and end apart: 2, of which 1 were waited for; matrix products, arithmetic and copies ran while one was open for 2% of the time, Pallas kernels for 0%

commit v1 on v0

--- a/solution.py
+++ b/solution.py
@@ -39,7 +39,7 @@
         lse = jnp.log(total)
         prob_sums.append(jnp.sum(probs, axis=1))
         square_sums.append(jnp.sum(lse * lse))
-        counts = lax.psum(local_counts(expert_ids[layer], experts), ("dp", "expert"))
+        counts = lax.psum(lax.psum(local_counts(expert_ids[layer], experts), "expert"), "dp")
         count_list.append(counts)
         share = counts / (tokens_all * picks)
         pull = balance_coef * experts * share

time: 159 us -> 140 us (0.88)
  blocking collectives: 82.1 us -> 62.1 us
    psum x1 -> x2, blocking collectives: 42 us -> 25.3 us  [the longest x1 13.5 us: on_device(): lax.psum(local_counts(expert_ids[layer], experts), 'expert')]
    psum x1, blocking collectives: 40 us -> 36.8 us  [on_device(): lax.psum((jnp.stack(prob_sums), jnp.stack(square_sums)), ('dp', 'expert'))]
where the time goes in v1:
time: 140 us; the launch traced here: 139 us
  blocking collectives  62.1 us (44%)
  waiting for transfers between devices  35.3 us (25%)
  matrix products  17.3 us (12%)
  between operations  14.2 us (10%)
  other arithmetic  7.88 us (6%)
  local copies, waits for them, and re-layouts  2.23 us (2%)
    psum x1, blocking collectives, on_device(): lax.psum((jnp.stack(prob_sums), jnp.stack(square_sums)), ('dp', 'expert'))  36.8 us
    psum x1, waiting for transfers between devices, on_device(): router_grad = lax.psum(columns, 'expert')  35.3 us
    psum x1, blocking collectives, on_device(): lax.psum(local_counts(expert_ids[layer], experts), 'expert')  13.5 us
    psum x1, blocking collectives, on_device(): lax.psum(lax.psum(local_counts(expert_ids[layer], experts), 'expert'), 'dp')  11.8 us
    dot_general x4, matrix products, on_device(): lax.dot_general(router_weight[layer], states, (((1,), (1,)), ((), ())), p...  9.21 us
    dot_general x4, matrix products, on_device(): term = jnp.dot(dlogits, states, preferred_element_type=jnp.float32)  8.06 us
  transfers between devices with their start and end apart: 2, of which 1 were waited for; matrix products, arithmetic and copies ran while one was open for 2% of the time, Pallas kernels for 0%

profile of v1, /device:TPU:0, one launch (start us, length us, event | category | flops | bytes accessed | tf_op | source)
XLA Modules:
  0.0 139.0 jit_solution(2781769687686042889)
XLA Ops:
  7.2 0.0 reduce-scatter.2.cloned.1.call-start
  7.2 2.3 %fusion.65 = (f32[256]{0:T(256)S(1)}, f32[8,256]{1,0:T(8,128)S(1)}) fusion(bf16[4,256,4096]{2,1,0:T(8,128)(2,1)} %param.3, bf16[4,8,4096]{2,1,0:T(8,128)(2,1)} %param.4), kind=kOutput, calls=%fused_computation.112 | convolution fusion | flops 16779008 | bytes 2171904 | tf_op jit(solution)/shard_map/dot_general | solution.py:30
  9.5 2.3 %fusion.66 = (f32[256]{0:T(256)S(1)}, f32[8,256]{1,0:T(8,128)S(1)}) fusion(bf16[4,256,4096]{2,1,0:T(8,128)(2,1)} %param.3, bf16[4,8,4096]{2,1,0:T(8,128)(2,1)} %param.4), kind=kOutput, calls=%fused_computation.113 | convolution fusion | flops 16779008 | bytes 2171904 | tf_op jit(solution)/shard_map/dot_general | solution.py:30
  11.8 2.3 %fusion.63 = (f32[256]{0:T(256)S(1)}, f32[8,256]{1,0:T(8,128)S(1)}) fusion(bf16[4,256,4096]{2,1,0:T(8,128)(2,1)} %param.3, bf16[4,8,4096]{2,1,0:T(8,128)(2,1)} %param.4), kind=kOutput, calls=%fused_computation.110 | convolution fusion | flops 16779008 | bytes 2171904 | tf_op jit(solution)/shard_map/dot_general | solution.py:30
  14.1 0.7 slice_bitcast_fusion.3
  14.9 0.1 convert_reduce_fusion.6
  15.0 0.1 convert_reduce_fusion.7
  15.1 0.1 convert_reduce_fusion.4
  15.2 0.1 convert_reduce_fusion.5
  15.4 0.1 convert_reduce_fusion
  15.5 0.1 convert_reduce_fusion.1
  15.6 0.1 convert_reduce_fusion.2
  15.7 0.1 convert_reduce_fusion.3
  15.9 2.3 %fusion.64 = (f32[256]{0:T(256)S(1)}, f32[8,256]{1,0:T(8,128)S(1)}) fusion(bf16[4,256,4096]{2,1,0:T(8,128)(2,1)} %param.3, bf16[4,8,4096]{2,1,0:T(8,128)(2,1)} %param.4), kind=kOutput, calls=%fused_computation.111 | convolution fusion | flops 16779008 | bytes 2171904 | tf_op jit(solution)/shard_map/dot_general | solution.py:30
  18.2 13.5 %all-reduce.2 = (f32[8]{0:T(128)S(1)}, f32[8]{0:T(128)S(1)}, f32[8]{0:T(128)S(1)}, f32[8]{0:T(128)S(1)}) all-reduce(f32[8]{0:T(128)S(1)} %add.54, f32[8]{0:T(128)S(1)} %add.52, f32[8]{0:T(128)S(1)} %add.50, f32[8]{0:T(128)S(1)} %add.48), channel_id=1, replica_groups=mesh['dp'=8,'expert'=4] {'expert'}, use_global_device_ids=true, to_apply=%region_21.0 | all-reduce | flops 32 | bytes 256 | tf_op jit(solution)/shard_map/psum | solution.py:42
  31.7 11.8 %all-reduce.1 = (f32[8]{0:T(128)S(1)}, f32[8]{0:T(128)S(1)}, f32[8]{0:T(128)S(1)}, f32[8]{0:T(128)S(1)}) all-reduce(f32[8]{0:T(128)S(1)} %get-tuple-element.16, f32[8]{0:T(128)S(1)} %get-tuple-element.17, f32[8]{0:T(128)S(1)} %get-tuple-element.18, f32[8]{0:T(128)S(1)} %get-tuple-element.19), channel_id=1, replica_groups=mesh['dp'=8,'expert'=4] {'dp'}, use_global_device_ids=true, to_apply=%region_22.0 | all-reduce | flops 32 | bytes 256 | tf_op jit(solution)/shard_map/psum | solution.py:42
  43.5 0.6 multiply_reduce_fusion.6
  44.1 0.7 multiply_reduce_fusion.7
  44.8 0.6 multiply_reduce_fusion.4
  45.4 0.6 multiply_reduce_fusion.5
  46.0 0.2 fusion.55
  46.2 2.0 %convolution_bitcast_fusion.3 = f32[1,8,4096]{2,1,0:T(8,128)S(1)} fusion(bf16[4,256,4096]{2,1,0:T(8,128)(2,1)} %param.3, f32[256]{0:T(256)S(1)} %get-tuple-element.33, f32[256]{0:T(256)S(1)} %get-tuple-element.3, f32[8]{0:T(128)S(1)} %broadcast_multiply_fusion.3, f32[8,256]{1,0:T(8,128)S(1)} %get-tuple-element.47, f32[256]{0:T(256)S(1)} %get-tuple-element.46), kind=kOutput, calls=%fused_computation.3 | convolution fusion | flops 16787456 | bytes 2239520 | tf_op jit(solution)/shard_map/dot_general | solution.py:49
  48.2 2.0 %convolution_bitcast_fusion.2 = f32[1,8,4096]{2,1,0:T(8,128)S(1)} fusion(bf16[4,256,4096]{2,1,0:T(8,128)(2,1)} %param.3, f32[256]{0:T(256)S(1)} %get-tuple-element.35, f32[256]{0:T(256)S(1)} %get-tuple-element.48, f32[8]{0:T(128)S(1)} %broadcast_multiply_fusion.2, f32[8,256]{1,0:T(8,128)S(1)} %get-tuple-element.45, f32[256]{0:T(256)S(1)} %get-tuple-element.44), kind=kOutput, calls=%fused_computation.2 | convolution fusion | flops 16787456 | bytes 2239520 | tf_op jit(solution)/shard_map/dot_general | solution.py:49
  50.2 0.2 fusion.57
  50.4 2.0 %convolution_bitcast_fusion.1 = f32[1,8,4096]{2,1,0:T(8,128)S(1)} fusion(bf16[4,256,4096]{2,1,0:T(8,128)(2,1)} %param.3, f32[256]{0:T(256)S(1)} %get-tuple-element.37, f32[256]{0:T(256)S(1)} %get-tuple-element.7, f32[8]{0:T(128)S(1)} %broadcast_multiply_fusion.1, f32[8,256]{1,0:T(8,128)S(1)} %get-tuple-element.43, f32[256]{0:T(256)S(1)} %get-tuple-element.42), kind=kOutput, calls=%fused_computation.1 | convolution fusion | flops 16787456 | bytes 2239520 | tf_op jit(solution)/shard_map/dot_general | solution.py:49
  52.4 2.0 %convolution_bitcast_fusion = f32[1,8,4096]{2,1,0:T(8,128)S(1)} fusion(bf16[4,256,4096]{2,1,0:T(8,128)(2,1)} %param.3, f32[256]{0:T(256)S(1)} %get-tuple-element.39, f32[256]{0:T(256)S(1)} %get-tuple-element.50, f32[8]{0:T(128)S(1)} %broadcast_multiply_fusion, f32[8,256]{1,0:T(8,128)S(1)} %get-tuple-element.41, f32[256]{0:T(256)S(1)} %get-tuple-element.40), kind=kOutput, calls=%fused_computation | convolution fusion | flops 16787456 | bytes 2239520 | tf_op jit(solution)/shard_map/dot_general | solution.py:49
  54.4 0.8 pad_maximum_fusion
  55.2 0.0 reduce-scatter.2.cloned.1.call-update
  55.2 0.0 all-reduce.5.cloned.1.call-start
  55.3 2.6 %pad_maximum_fusion.3 = f32[4]{0:T(128)S(1)} fusion(f32[1]{0:T(128)} %bitcast.36, f32[1]{0:T(128)} %bitcast.35, f32[1]{0:T(128)} %bitcast.34, f32[1]{0:T(128)} %bitcast.33), kind=kLoop, calls=%fused_computation.95 | loop fusion | flops 12 | bytes 32 | tf_op jit(solution)/shard_map/stack | solution.py:54
  57.9 36.8 %all-reduce = (f32[4]{0:T(128)S(1)}, f32[4,8]{1,0:T(4,128)S(1)}) all-reduce(f32[4]{0:T(128)S(1)} %pad_maximum_fusion.3, f32[4,8]{1,0:T(4,128)S(1)} %pad_maximum_fusion.1), channel_id=1, replica_groups=mesh['dp'=8,'expert'=4] {'dp','expert'}, use_global_device_ids=true, to_apply=%region_36.0 | all-reduce | flops 36 | bytes 288 | tf_op jit(solution)/shard_map/psum | solution.py:53
  94.7 0.1 fusion.54
  94.8 0.0 reduce-scatter.2.cloned.1.call-done
  94.9 0.0 all-reduce.5.cloned.1.call-update
  94.9 0.6 pad_maximum_fusion.2
  95.5 35.3 %all-reduce.5.cloned.1.call-done = f32[4,8,512]{2,1,0:T(8,128)} async-done(((f32[4,8,512]{2,1,0:T(8,128)}), f32[4,8,512]{2,1,0:T(8,128)}) %all-reduce.5.cloned.1.call-update) | async-done | bytes 65552 | tf_op jit(solution)/shard_map/psum | solution.py:52
  130.7 1.5 %copy.6 = f32[4,8,512]{2,1,0:T(8,128)} copy(f32[4,8,512]{2,1,0:T(8,128)} %all-reduce.5.cloned.1.call-done) | data formatting | bytes 131072
  (15 shorter events, 0.1 us)
Async XLA Ops:
  7.2 87.7 %reduce-scatter.2.cloned.1.call-start = ((), (), s32[]{:S(2)}) async-start(), calls=%async_computation.1 | async-start | bytes 589824 | tf_op jit(solution)/shard_map/reduce_scatter | solution.py:51
  55.2 75.5 %all-reduce.5.cloned.1.call-start = ((), (), s32[]{:S(2)}) async-start(), calls=%async_computation.2 | async-start | bytes 131072 | tf_op jit(solution)/shard_map/psum | solution.py:52
Sparse Core Ops, SparseCore 0:
  55.4 31.4 reduce-scatter.1
  95.0 35.6 all-reduce.4
